TPU v7x, 16 devices: a whole 2x2x2 slice. The times are simulated.
16 devices in a mesh: dp: 1, tp: 16 (over x, y, z, core).
Axes of the slice: x: 2, y: 2, z: 2, core: 2. Of those that a mesh axis runs over, the one named last changes fastest.
Arguments:
- x: bfloat16 [5632, 3072], P(('dp', 'tp'))
- w: bfloat16 [3072, 32768], P(None, 'tp')
- label: int32 [5632], P(('dp', 'tp'))
Outputs:
- output 1: float32 [5632], P(('dp', 'tp'))
- output 2: bfloat16 [5632, 3072], P(('dp', 'tp'))
- output 3: bfloat16 [3072, 32768], P('dp', 'tp')
All inputs are finite; a program needn't handle non-finite values.
Results may differ from a plain program's by a relative error of at most 0.012.
Values are sent between devices in bfloat16 or wider.
A program may use at most 2 GiB of HBM per device.

v0:
```python
import jax
import jax.numpy as jnp
from jax import lax
from jax.sharding import PartitionSpec as P


def solution(mesh):
    def step(x, w, label):
        me, own_rows, columns = lax.axis_index("tp"), x.shape[0], w.shape[1]
        rows = lax.all_gather(x, "tp", axis=0, tiled=True)
        wanted = lax.all_gather(label, "tp", axis=0, tiled=True)
        logits = jnp.dot(rows, w, preferred_element_type=jnp.float32)
        hit = (wanted - me * columns)[:, None] == jnp.arange(columns, dtype=jnp.int32)[None, :]
        high = jnp.max(logits, -1)
        own = jnp.stack([high, jnp.sum(jnp.exp(logits - high[:, None]), -1), jnp.sum(jnp.where(hit, logits, 0.0), -1)])
        high, sums, right = jnp.moveaxis(lax.all_gather(own, "tp"), 1, 0)
        top = jnp.max(high, 0)
        total = jnp.sum(sums * jnp.exp(high - top), 0)
        loss = jnp.log(total) + top - jnp.sum(right, 0)
        e = jnp.exp(logits - top[:, None])
        by_logits = (e / total[:, None] - hit.astype(jnp.float32)).astype(jnp.bfloat16)
        term = jnp.dot(by_logits, w.T, preferred_element_type=jnp.float32).astype(jnp.bfloat16)
        by_x = lax.psum_scatter(term, "tp", scatter_dimension=0, tiled=True)
        by_w = jnp.dot(rows.T, by_logits, preferred_element_type=jnp.float32).astype(jnp.bfloat16)
        return lax.dynamic_slice_in_dim(loss, me * own_rows, own_rows), by_x, by_w

    return jax.shard_map(
        step,
        mesh=mesh,
        in_specs=(P(("dp", "tp"), None), P(None, "tp"), P(("dp", "tp"))),
        out_specs=(P(("dp", "tp")), P(("dp", "tp"), None), P("dp", "tp")),
        check_vma=False,
    )
```

profile of v0, /device:TPU:0, one launch (start us, length us, event | category | flops | bytes accessed | tf_op | source)
XLA Modules:
  0.0 588.0 jit_solution(16313442427501958133)
XLA Ops:
  7.2 0.0 all-gather.5.cloned.1.call-start
  7.2 0.7 all-gather.5.cloned.1.call-update
  7.9 0.0 all-gather.7.cloned.1.call-start
  8.0 0.9 dynamic-update-slice
  8.9 35.5 %all-reduce = s32[5632]{0:T(1024)S(1)} all-reduce(s32[5632]{0:T(1024)S(1)} %dynamic-update-slice), channel_id=1, replica_groups=mesh['dp'=1,'tp'=16] {'tp'}, use_global_device_ids=true, to_apply=%add | all-reduce | flops 5632 | bytes 45056
  44.3 0.6 broadcast_subtract_fusion
  45.0 103.4 %all-gather.5.cloned.1.call-done = bf16[5632,3072]{1,0:T(8,128)(2,1)} async-done(((bf16[352,3072]{1,0:T(8,128)(2,1)}), bf16[5632,3072]{1,0:T(8,128)(2,1)}) %all-gather.5.cloned.1.call-update) | async-done | bytes 34603024 | tf_op jit(solution)/shard_map/all_gather | solution.py:10
  148.3 82.1 %fusion.3 = (f32[5632]{0:T(1024)S(1)}, f32[5632,2048]{0,1:T(8,128)}) fusion(bf16[5632,3072]{1,0:T(8,128)(2,1)} %all-gather.5.cloned.1.call-done, bf16[3072,2048]{1,0:T(8,128)(2,1)} %param.4), kind=kOutput, calls=%fused_computation.18 | convolution fusion | flops 70878486528 | bytes 93345792 | tf_op jit(solution)/shard_map/dot_general | solution.py:12
  230.4 0.0 copy-done.1
  230.4 20.5 %exponential_reduce_fusion = (f32[5632]{0:T(1024)S(1)}, f32[5632]{0:T(1024)S(1)}) fusion(f32[5632,2048]{0,1:T(8,128)} %get-tuple-element.16, f32[5632]{0:T(1024)S(1)} %get-tuple-element.15, s32[5632]{0:T(1024)S(1)} %copy-done.1), kind=kLoop, calls=%fused_computation.3 | loop fusion | flops 57660416 | bytes 46227456 | tf_op jit(solution)/shard_map/reduce_sum | solution.py:15
  251.0 0.7 maximum_bitcast_fusion
  251.7 0.0 all-gather.7.cloned.1.call-update
  251.7 0.2 reduce-scatter.2.cloned.1.call-start
  251.9 26.4 %all-gather.7.cloned.1.call-done = f32[16,3,5632]{2,1,0:T(4,128)} async-done(((f32[1,3,5632]{2,1,0:T(4,128)}), f32[16,3,5632]{2,1,0:T(4,128)}) %all-gather.7.cloned.1.call-update) | async-done | bytes 1081360 | tf_op jit(solution)/shard_map/all_gather | solution.py:16
  278.3 4.2 slice_reduce_fusion.1
  282.5 0.1 fusion.1
  282.6 29.1 %subtract_convert_fusion = bf16[5632,2048]{0,1:T(8,128)(2,1)} fusion(f32[5632,2048]{0,1:T(8,128)} %get-tuple-element.16, f32[5632]{0:T(1024)S(1)} %fusion.1, f32[5632]{0:T(1024)S(1)} %get-tuple-element.11, s32[5632]{0:T(1024)S(1)} %copy-done.1), kind=kLoop, calls=%fused_computation | loop fusion | flops 69206016 | bytes 69273600 | tf_op jit(solution)/shard_map/convert_element_type | solution.py:21
  311.7 0.0 copy-done.2
  311.7 80.3 %convolution_convert_fusion = bf16[5632,3072]{1,0:T(8,128)(2,1)} fusion(bf16[5632,2048]{0,1:T(8,128)(2,1)} %subtract_convert_fusion, bf16[3072,2048]{1,0:T(8,128)(2,1)} %param.4), kind=kOutput, calls=%fused_computation.4 | convolution fusion | flops 70884261888 | bytes 70254592 | tf_op jit(solution)/shard_map/dot_general | solution.py:22
  392.1 0.0 reduce-scatter.2.cloned.1.call-update
  392.1 81.6 %convert_bitcast_fusion = bf16[3072,2048]{0,1:T(8,128)(2,1)} fusion(bf16[5632,2048]{0,1:T(8,128)(2,1)} %subtract_convert_fusion, bf16[5632,3072]{1,0:T(8,128)(2,1)} %all-gather.5.cloned.1.call-done), kind=kOutput, calls=%fused_computation.5 | convolution fusion | flops 70873251840 | bytes 70254592 | tf_op jit(solution)/shard_map/dot_general | solution.py:24
  473.7 16.6 %copy.9 = bf16[3072,2048]{1,0:T(8,128)(2,1)} copy(bf16[3072,2048]{0,1:T(8,128)(2,1)} %convert_bitcast_fusion) | data formatting | bytes 25165824
  490.3 1.4 dynamic-slice_subtract_fusion
  491.7 89.8 %reduce-scatter.2.cloned.1.call-done = bf16[352,3072]{1,0:T(8,128)(2,1)} async-done(((bf16[5632,3072]{1,0:T(8,128)(2,1)}), bf16[352,3072]{1,0:T(8,128)(2,1)}) %reduce-scatter.2.cloned.1.call-update) | async-done | bytes 2162704 | tf_op jit(solution)/shard_map/reduce_scatter | solution.py:23
  (8 shorter events, 0.1 us)
Async XLA Ops:
  7.2 141.2 %all-gather.5.cloned.1.call-start = ((), (), s32[]{:S(2)}) async-start(), calls=%async_computation.1 | async-start | bytes 36765696 | tf_op jit(solution)/shard_map/all_gather | solution.py:10
  7.9 270.4 %all-gather.7.cloned.1.call-start = ((), (), s32[]{:S(2)}) async-start(), calls=%async_computation.3 | async-start | bytes 1531904 | tf_op jit(solution)/shard_map/all_gather | solution.py:16
  148.3 82.1 %copy-start.1 = (s32[5632]{0:T(1024)S(1)}, s32[5632]{0:T(1024)}, u32[]{:S(2)}) copy-start(s32[5632]{0:T(1024)} %broadcast_subtract_fusion) | copy-start | bytes 67588
  251.7 329.8 %reduce-scatter.2.cloned.1.call-start = ((), (), s32[]{:S(2)}) async-start(), calls=%async_computation.2 | async-start | bytes 36765696 | tf_op jit(solution)/shard_map/reduce_scatter | solution.py:23
  282.5 29.2 %copy-start = (f32[5632]{0:T(1024)}, f32[5632]{0:T(1024)S(1)}, u32[]{:S(2)}) copy-start(f32[5632]{0:T(1024)S(1)} %get-tuple-element.11) | copy-start | bytes 67588
  282.6 29.1 %copy-start.2 = (f32[5632]{0:T(1024)}, f32[5632]{0:T(1024)S(1)}, u32[]{:S(2)}) copy-start(f32[5632]{0:T(1024)S(1)} %fusion.1) | copy-start | bytes 67588
Sparse Core Ops, SparseCore 0:
  10.2 138.0 all-gather.4
  251.8 26.4 all-gather.6
  392.2 189.2 reduce-scatter.1
where the time goes:
time: 589 us; the launch traced here: 588 us
  matrix products  244 us (41%)
  waiting for transfers between devices  220 us (37%)
  other arithmetic  56.6 us (10%)
  blocking collectives  35.5 us (6%)
  local copies, waits for them, and re-layouts  17.6 us (3%)
  between operations  13.8 us (2%)
    all_gather x1, waiting for transfers between devices, step(): rows = lax.all_gather(x, 'tp', axis=0, tiled=True)  103 us
    reduce_scatter x1, waiting for transfers between devices, step(): by_x = lax.psum_scatter(term, 'tp', scatter_dimension=0, tiled=True)  89.8 us
    dot_general x1, matrix products, step(): logits = jnp.dot(rows, w, preferred_element_type=jnp.float32)  82.1 us
    dot_general x1, matrix products, step(): jnp.dot(rows.T, by_logits, preferred_element_type=jnp.float32)  81.6 us
    dot_general x1, matrix products, step(): jnp.dot(by_logits, w.T, preferred_element_type=jnp.float32)  80.3 us
    unnamed x1, blocking collectives  35.5 us
    convert_element_type x1, other arithmetic, step(): (e / total[:, None] - hit.astype(jnp.float32)).astype(jnp.bfloat16)  29.1 us
    all_gather x1, waiting for transfers between devices, step(): high, sums, right = jnp.moveaxis(lax.all_gather(own, 'tp'), 1, 0)  26.4 us
  transfers between devices with their start and end apart: 3, of which 3 were waited for; matrix products, arithmetic and copies ran while one was open for 17% of the time, Pallas kernels for 0%

commit v1 on v0

v1 whole, which is shorter than its diff:
```python
import jax
import jax.numpy as jnp
from jax import lax
from jax.experimental import pallas as pl
from jax.experimental.pallas import tpu as pltpu
from jax.sharding import PartitionSpec as P

F32, BF16, I32 = jnp.float32, jnp.bfloat16, jnp.int32
R, D, C = 352, 3072, 2048
PO, PS = (0, 128, 240), (128, 112, 112)
AXES = (8, 4, 2)
NB = 16
MB = 256
DONE = 6
VMEM_LIMIT = 67_000_000


def flip(me, v):
    return v * (1 - 2 * ((me // v) % 2))


def place():
    me = lax.axis_index("tp")
    return me, me + flip(me, 1), [me + flip(me, v) for v in AXES]


def origin(me, s, k, j):
    q = me + k * flip(me, 1)
    for b in range(3):
        q = q + ((s // (1 << b)) % 2) * flip(me, AXES[(j + b) % 3])
    return q


def order(i):
    return jnp.where(i == 3, 4, jnp.where(i == 4, 3, i))


def rc(src, dst, ss, rs, dev):
    return pltpu.make_async_remote_copy(
        src_ref=src, dst_ref=dst, send_sem=ss, recv_sem=rs, device_id={"tp": dev}, device_id_type=pl.DeviceIdType.MESH
    )


def rows(j):
    return pl.ds(PO[j], PS[j])


def eye():
    return lax.broadcasted_iota(I32, (128, 128), 0) == lax.broadcasted_iota(I32, (128, 128), 1)


def to_column(row):
    return jnp.sum(jnp.where(eye(), row, 0.0), 1, keepdims=True)


def to_row(column, n):
    return jnp.sum(jnp.where(eye()[:n], column, 0.0), 0, keepdims=True)


def fill_columns(dst, tile, j, row, shift=0.0):
    col = to_column(tile[row : row + 1, :].astype(F32) - shift)
    dst[rows(j), :] = jnp.broadcast_to(col, (128, 128))[: PS[j]]


def first_kernel(
    x_hbm, w_hbm, lab_ref,
    z_hbm, xr_hbm, loss_ref, st_out, lab_out,
    xv, w, zb, labc, mc, sc, rcol, stile, strecv, st_all, lab_all,
    isend, irecv, dsend, drecv, zsem, xsem, lsend, lrecv, ssend, srecv, tsend, trecv, insem,
):
    me, partner, nbr = place()
    base = me * C
    load_x = pltpu.make_async_copy(x_hbm, xv.at[0, 0], insem.at[0])
    load_w = pltpu.make_async_copy(w_hbm, w, insem.at[1])
    load_x.start()
    load_w.start()

    barrier = pltpu.get_barrier_semaphore()

    @pl.loop(1, NB)
    def _(t):
        pl.semaphore_signal(barrier, inc=1, device_id={"tp": (me + t) % NB}, device_id_type=pl.DeviceIdType.MESH)

    pl.semaphore_wait(barrier, NB - 1)

    def label_copy(t):
        return rc(lab_ref, lab_all.at[me], lsend.at[t], lrecv.at[me], (me + t) % NB)

    def label_from(t):
        q = (me + t) % NB
        return rc(lab_ref, lab_all.at[q], lsend.at[t], lrecv.at[q], q)

    def ici(s, b, j):
        t = s + (1 << b)
        return rc(xv.at[s, 0, rows(j)], xv.at[t, 0, rows(j)], isend.at[t, j], irecv.at[t, j], nbr[(j + b) % 3])

    def d2d(s):
        return rc(xv.at[s, 0], xv.at[s, 1], dsend.at[s], drecv.at[s], partner)

    def z_out(s, k, par):
        return pltpu.make_async_copy(zb.at[par], z_hbm.at[pl.ds((2 * s + k) * R, R)], zsem.at[par])

    def x_out(s, k):
        return pltpu.make_async_copy(xv.at[s, k], xr_hbm.at[pl.ds((2 * s + k) * R, R)], xsem.at[s, k])

    def stat_copy(s, k, j):
        n = 2 * s + k
        q = origin(me, s, k, j)
        return rc(stile.at[n, j], strecv.at[me, j], ssend.at[n, j], srecv.at[me, j], q)

    @pl.loop(1, NB)
    def _(t):
        label_copy(t).start()

    lab_all[me] = lab_ref[...]
    load_x.wait()

    @pl.loop(0, 8)
    def _(i):
        s = order(i)
        for k in range(2):
            if k == 0:

                @pl.when(i > 0)
                def _():
                    for j in range(3):
                        rc(xv.at[s, 0, rows(j)], xv.at[s, 0, rows(j)], isend.at[s, j], irecv.at[s, j], nbr[j]).wait_recv()

                for b in range(3):

                    @pl.when(s < (1 << b))
                    def _():
                        for j in range(3):
                            ici(s, b, j).start()

                d2d(s).start()

                @pl.when(i == 0)
                def _():
                    load_w.wait()

                    @pl.loop(1, NB)
                    def _(t):
                        label_from(t).wait_recv()
            else:
                d2d(s).wait_recv()
            x_out(s, k).start()

            @pl.when(i > 0)
            def _():
                z_out(0, k, k).wait()

            zb[k] = jnp.dot(xv[s, k], w[...], preferred_element_type=F32)
            for j in range(3):
                fill_columns(labc, lab_all[origin(me, s, k, j)], j, j, base.astype(F32))

            @pl.loop(0, 4)
            def _(n):
                r = pl.ds(pl.multiple_of(n * 88, 8), 88)
                high = zb[k, r, 0:128]
                for c in range(1, C // 128):
                    high = jnp.maximum(high, zb[k, r, c * 128 : (c + 1) * 128])
                high = jnp.max(high, 1, keepdims=True)
                lab = labc[r, :]
                lane = lax.broadcasted_iota(I32, (88, 128), 1).astype(F32)
                sums = jnp.zeros((88, 128), F32)
                right = jnp.zeros((88, 128), F32)
                for c in range(C // 128):
                    z = zb[k, r, c * 128 : (c + 1) * 128]
                    sums = sums + jnp.exp(z - high)
                    right = right + jnp.where(lane == lab - c * 128.0, z, 0.0)
                mc[r, :] = jnp.broadcast_to(high, (88, 128))
                sc[r, :] = jnp.broadcast_to(jnp.sum(sums, 1, keepdims=True), (88, 128))
                rcol[r, :] = jnp.broadcast_to(jnp.sum(right, 1, keepdims=True), (88, 128))

            z_out(s, k, k).start()
            for j in range(3):
                for n, ref in enumerate((mc, sc, rcol)):
                    stile[2 * s + k, j, n : n + 1, :] = to_row(ref[rows(j), :], PS[j])
            if k == 0:

                @pl.when(i == 0)
                def _():
                    for j in range(3):
                        strecv[me, j] = stile[0, j]

                @pl.when(i > 0)
                def _():
                    for j in range(3):
                        stat_copy(s, k, j).start()
            else:
                for j in range(3):
                    stat_copy(s, k, j).start()

    @pl.loop(1, NB)
    def _(t):
        q = (me + t) % NB
        for j in range(3):
            rc(strecv.at[q, j], strecv.at[q, j], ssend.at[0, j], srecv.at[q, j], q).wait_recv()

    for j in range(3):
        tiles = [strecv[q, j] for q in range(NB)]
        top = tiles[0][0:1]
        for t in tiles[1:]:
            top = jnp.maximum(top, t[0:1])
        total = jnp.zeros((1, 128), F32)
        right = jnp.zeros((1, 128), F32)
        for t in tiles:
            total = total + t[1:2] * jnp.exp(t[0:1] - top)
            right = right + t[2:3]
        loss_ref[j : j + 1, :] = jnp.log(total) + top - right
        st_all[me, j : j + 1, :] = top
        st_all[me, j + 3 : j + 4, :] = 1.0 / total

    def top_copy(t):
        return rc(st_all.at[me], st_all.at[me], tsend.at[t], trecv.at[me], (me + t) % NB)

    def top_from(t):
        q = (me + t) % NB
        return rc(st_all.at[q], st_all.at[q], tsend.at[t], trecv.at[q], q)

    @pl.loop(1, NB)
    def _(t):
        top_copy(t).start()

    lab_out[...] = lab_all[...]
    for s in range(8):
        for k in range(2):
            x_out(s, k).wait()
    for k in range(2):
        z_out(0, k, k).wait()
    for b in range(3):
        for s in range(1 << b):
            for j in range(3):
                ici(s, b, j).wait_send()

    @pl.loop(0, 8)
    def _(s):
        d2d(s).wait_send()

    @pl.loop(1, NB)
    def _(n):
        for j in range(3):
            stat_copy(n // 2, n % 2, j).wait_send()

    @pl.loop(1, NB)
    def _(t):
        label_copy(t).wait_send()
        top_copy(t).wait_send()
        top_from(t).wait_recv()

    st_out[...] = st_all[...]


def by_w_block(xb, g, ob):
    for c in range(4):
        ob[:, c * 512 : (c + 1) * 512] = lax.dot_general(
            xb[...], g[:, c * 512 : (c + 1) * 512], (((0,), (0,)), ((), ())), preferred_element_type=F32
        ).astype(BF16)


def second_kernel(
    z_hbm, xr_hbm, w_hbm, st_ref, lab_ref,
    byx, g_hbm, bw, dbuf, ibuf,
    w, g, zin, pool, acc, xb, ob, topc, invc, labc,
    insem, zsem, dsend, drecv, isend, irecv, gsem, lsem, xsem, osem,
):
    me, partner, nbr = place()
    base = me * C
    load_w = pltpu.make_async_copy(w_hbm, w, insem.at[0])

    def z_in(s, k, h):
        return pltpu.make_async_copy(z_hbm.at[pl.ds((2 * s + k) * R + h * 88, 88)], zin.at[h % 2], zsem.at[h % 2])

    z_in(7, 1, 0).start()
    z_in(7, 1, 1).start()
    load_w.start()
    barrier = pltpu.get_barrier_semaphore()
    for q in (partner, *nbr):
        pl.semaphore_signal(barrier, inc=1, device_id={"tp": q}, device_id_type=pl.DeviceIdType.MESH)
    pl.semaphore_wait(barrier, 4)

    def d2d(s, p):
        return rc(pool.at[p], dbuf.at[s], dsend.at[p], drecv.at[s], partner)

    def ici(s, b, p, j):
        return rc(pool.at[p, rows(j)], ibuf.at[s, rows(j)], isend.at[p, j], irecv.at[s, j], nbr[(j + b) % 3])

    def fetch(src, p):
        return pltpu.make_async_copy(src, pool.at[p], lsem.at[p])

    def g_out(s, k):
        n = pl.ds((2 * s + k) * R, R)
        return pltpu.make_async_copy(g.at[n], g_hbm.at[n], gsem.at[s, k])

    def x_in(m):
        return pltpu.make_async_copy(xr_hbm.at[:, pl.ds(m * MB, MB)], xb.at[m % 2], xsem.at[m % 2])

    def bw_out(m):
        return pltpu.make_async_copy(ob.at[m % 2], bw.at[pl.ds(m * MB, MB)], osem.at[m % 2])

    def gradient(s, k, nxt):
        for j in range(3):
            q = origin(me, s, k, j)
            fill_columns(topc, st_ref[q], j, j)
            fill_columns(invc, st_ref[q], j, j + 3)
            fill_columns(labc, lab_ref[q], j, j, base.astype(F32))

        @pl.loop(0, 4)
        def _(h):
            z_in(s, k, h).wait()
            r = pl.ds(pl.multiple_of(h * 88, 8), 88)
            to = pl.ds(pl.multiple_of((2 * s + k) * R + h * 88, 8), 88)
            top, inv, lab = topc[r, :], invc[r, :], labc[r, :]
            lane = lax.broadcasted_iota(I32, (88, 128), 1).astype(F32)
            for c in range(C // 128):
                e = jnp.exp(zin[h % 2, :, c * 128 : (c + 1) * 128] - top) * inv
                hit = jnp.where(lane == lab - c * 128.0, 1.0, 0.0)
                g[to, c * 128 : (c + 1) * 128] = (e - hit).astype(BF16)

            @pl.when(h < 2)
            def _():
                z_in(s, k, h + 2).start()

            @pl.when(h >= 2)
            def _():
                nxt(h - 2)

        g_out(s, k).start()

    def term(s, k, n):
        return lax.dot_general(
            g[pl.ds(pl.multiple_of((2 * s + k) * R, R), R), :],
            w[pl.ds(pl.multiple_of(n * 1536, 1536), 1536), :],
            (((1,), (1,)), ((), ())),
            preferred_element_type=F32,
        )

    def wait_slot(s):
        for j in range(3):
            rc(ibuf.at[s, rows(j)], ibuf.at[s, rows(j)], isend.at[2, j], irecv.at[s, j], nbr[j]).wait_recv()

    @pl.loop(0, 8)
    def _(i):
        s = 7 - order(i)
        prev = 7 - order(jnp.maximum(i - 1, 0))
        after = 7 - order(jnp.minimum(i + 1, 7))
        a = i % 2
        p = 2 + (i + 2) % 3

        def next_half(h):
            z_in(s, 0, h).start()

        def next_slot(h):
            @pl.when(i < 7)
            def _():
                z_in(after, 1, h).start()

        gradient(s, 1, next_half)

        @pl.when(i == 0)
        def _():
            load_w.wait()

        @pl.when(i > 1)
        def _():
            d2d(0, a).wait_send()

        @pl.when(i > 3)
        def _():
            for j in range(3):
                ici(0, 0, p, j).wait_send()

        @pl.when(i > 0)
        def _():
            d2d(prev, 0).wait_recv()
            fetch(dbuf.at[prev], 5).start()

            @pl.when(prev < 4)
            def _():
                wait_slot(prev + 4)
                fetch(ibuf.at[prev + 4], 6).start()

            @pl.when(prev < 2)
            def _():
                wait_slot(prev + 2)
                fetch(ibuf.at[prev + 2], p).start()

        @pl.loop(0, 2)
        def _(n):
            c = pl.ds(pl.multiple_of(n * 1536, 1536), 1536)
            pool[a, :, c] = term(s, 1, n).astype(BF16)

        d2d(s, a).start()
        gradient(s, 0, next_slot)

        @pl.when(i > 0)
        def _():
            fetch(dbuf.at[prev], 5).wait()

            @pl.when(prev < 4)
            def _():
                fetch(ibuf.at[prev + 4], 6).wait()

            @pl.when(prev < 2)
            def _():
                fetch(ibuf.at[prev + 2], p).wait()

            @pl.loop(0, 2)
            def _(n):
                c = pl.ds(pl.multiple_of(n * 1536, 1536), 1536)
                acc[...] = term(prev, 0, n) + pool[5, :, c].astype(F32)

                @pl.when(prev < 4)
                def _():
                    acc[...] += pool[6, :, c].astype(F32)

                @pl.when(prev < 2)
                def _():
                    acc[...] += pool[p, :, c].astype(F32)

                pool[p, :, c] = acc[...].astype(BF16)

            @pl.when(prev >= 4)
            def _():
                for j in range(3):
                    ici(prev, 2, p, j).start()

            @pl.when((prev >= 2) & (prev < 4))
            def _():
                for j in range(3):
                    ici(prev, 1, p, j).start()

            @pl.when(prev == 1)
            def _():
                for j in range(3):
                    ici(prev, 0, p, j).start()

    x_in(0).start()
    x_in(1).start()

    @pl.loop(0, DONE)
    def _(m):
        x_in(m).wait()

        @pl.when(m > 1)
        def _():
            bw_out(m - 2).wait()

        by_w_block(xb.at[m % 2], g, ob.at[m % 2])
        bw_out(m).start()

        @pl.when(m + 2 < DONE)
        def _():
            x_in(m + 2).start()

    for a in range(2):
        d2d(0, a).wait_send()
    d2d(0, 0).wait_recv()
    fetch(dbuf.at[0], 5).start()
    for s, p in ((4, 6), (2, 0), (1, 1)):
        wait_slot(s)
        fetch(ibuf.at[s], p).start()
    for p in (5, 6, 0, 1):
        fetch(dbuf.at[0], p).wait()

    @pl.loop(0, 2)
    def _(n):
        c = pl.ds(pl.multiple_of(n * 1536, 1536), 1536)
        acc[...] = term(0, 0, n)
        for p in (5, 6, 0, 1):
            acc[...] += pool[p, :, c].astype(F32)
        pool[5, :, c] = acc[...].astype(BF16)

    out = pltpu.make_async_copy(pool.at[5], byx, lsem.at[5])
    out.start()
    out.wait()

    for p in (2, 3, 4):
        for j in range(3):
            ici(0, 0, p, j).wait_send()
    for s in range(8):
        for k in range(2):
            g_out(s, k).wait()
    for m in (DONE - 2, DONE - 1):
        bw_out(m).wait()


def third_kernel(g_hbm, xr_hbm, part_hbm, bw, g, xb, ob, part, acc, gsem, xsem, osem, psem):
    blocks = D // MB

    def g_in(n):
        r = pl.ds(n * 1408, 1408)
        return pltpu.make_async_copy(g_hbm.at[r], g.at[r], gsem.at[n])

    def x_in(m):
        return pltpu.make_async_copy(xr_hbm.at[:, pl.ds(m * MB, MB)], xb.at[m % 2], xsem.at[m % 2])

    def bw_out(m):
        return pltpu.make_async_copy(ob.at[m % 2], bw.at[pl.ds(m * MB, MB)], osem.at[m % 2])

    p_in = pltpu.make_async_copy(part_hbm, part, psem.at[0])
    p_out = pltpu.make_async_copy(part, bw.at[pl.ds(0, DONE * MB)], psem.at[1])
    x_in(DONE).start()
    for n in range(4):
        g_in(n).start()
    x_in(DONE + 1).start()
    p_in.start()

    x_in(DONE).wait()
    for n in range(4):
        g_in(n).wait()
        r = pl.ds(n * 1408, 1408)
        for c in range(4):
            cols = pl.ds(c * 512, 512)
            t = lax.dot_general(
                xb[DONE % 2, r, :], g[r, cols], (((0,), (0,)), ((), ())), preferred_element_type=F32
            )
            if n == 0:
                acc[:, cols] = t
            else:
                acc[:, cols] += t
    ob[DONE % 2] = acc[...].astype(BF16)
    bw_out(DONE).start()
    x_in(DONE + 2).start()
    p_in.wait()
    p_out.start()

    @pl.loop(DONE + 1, blocks)
    def _(m):
        x_in(m).wait()

        @pl.when(m > DONE + 1)
        def _():
            bw_out(m - 2).wait()

        by_w_block(xb.at[m % 2], g, ob.at[m % 2])
        bw_out(m).start()

        @pl.when(m + 2 < blocks)
        def _():
            x_in(m + 2).start()

    for m in (blocks - 2, blocks - 1):
        bw_out(m).wait()
    p_out.wait()


ANY = pl.BlockSpec(memory_space=pl.ANY)
VM = pl.BlockSpec(memory_space=pltpu.VMEM)


def params(n=None):
    if n is None:
        return pltpu.CompilerParams(vmem_limit_bytes=VMEM_LIMIT)
    return pltpu.CompilerParams(vmem_limit_bytes=VMEM_LIMIT, collective_id=n, has_side_effects=True)


def S(shape, dtype):
    return jax.ShapeDtypeStruct(shape, dtype)


def pieces(v):
    out = [jnp.pad(v[o : o + n], (0, 128 - n)) for o, n in zip(PO, PS)]
    return jnp.pad(jnp.stack(out), ((0, 5), (0, 0)))


def solution(mesh):
    DMA = pltpu.SemaphoreType.DMA
    rows_all = NB * R

    def step(x, w, label):
        z, xr, loss, st, lab = pl.pallas_call(
            first_kernel,
            out_shape=(
                S((rows_all, C), F32),
                S((rows_all, D), BF16),
                S((8, 128), F32),
                S((NB, 8, 128), F32),
                S((NB, 8, 128), I32),
            ),
            in_specs=[ANY, ANY, VM],
            out_specs=(ANY, ANY, VM, VM, VM),
            scratch_shapes=[
                pltpu.VMEM((8, 2, R, D), BF16),
                pltpu.VMEM((D, C), BF16),
                pltpu.VMEM((2, R, C), F32),
                pltpu.VMEM((R, 128), F32),
                pltpu.VMEM((R, 128), F32),
                pltpu.VMEM((R, 128), F32),
                pltpu.VMEM((R, 128), F32),
                pltpu.VMEM((NB, 3, 8, 128), F32),
                pltpu.VMEM((NB, 3, 8, 128), F32),
                pltpu.VMEM((NB, 8, 128), F32),
                pltpu.VMEM((NB, 8, 128), I32),
                DMA((8, 3)), DMA((8, 3)), DMA((8,)), DMA((8,)), DMA((2,)), DMA((8, 2)),
                DMA((NB,)), DMA((NB,)), DMA((NB, 3)), DMA((NB, 3)), DMA((NB,)), DMA((NB,)), DMA((2,)),
            ],
            compiler_params=params(0),
            cost_estimate=pl.CostEstimate(flops=2 * rows_all * D * C, bytes_accessed=120_000_000, transcendentals=rows_all * C),
            name="gather_logits",
        )(x, w, pieces(label))

        byx, g, part, _, _ = pl.pallas_call(
            second_kernel,
            out_shape=(
                S((R, D), BF16),
                S((rows_all, C), BF16),
                S((DONE * MB, C), BF16),
                S((8, R, D), BF16),
                S((8, R, D), BF16),
            ),
            in_specs=[ANY, ANY, ANY, VM, VM],
            out_specs=(ANY, ANY, ANY, ANY, ANY),
            scratch_shapes=[
                pltpu.VMEM((D, C), BF16),
                pltpu.VMEM((rows_all, C), BF16),
                pltpu.VMEM((2, 88, C), F32),
                pltpu.VMEM((7, R, D), BF16),
                pltpu.VMEM((R, 1536), F32),
                pltpu.VMEM((2, rows_all, MB), BF16),
                pltpu.VMEM((2, MB, C), BF16),
                pltpu.VMEM((R, 128), F32),
                pltpu.VMEM((R, 128), F32),
                pltpu.VMEM((R, 128), F32),
                DMA((1,)), DMA((2,)), DMA((2,)), DMA((8,)), DMA((5, 3)), DMA((8, 3)), DMA((8, 2)), DMA((8,)), DMA((2,)), DMA((2,)),
            ],
            compiler_params=params(1),
            cost_estimate=pl.CostEstimate(flops=3 * rows_all * D * C, bytes_accessed=200_000_000, transcendentals=rows_all * C),
            name="scatter_terms",
        )(z, xr, w, st, lab)

        by_w = pl.pallas_call(
            third_kernel,
            out_shape=S((D, C), BF16),
            in_specs=[ANY, ANY, ANY],
            out_specs=ANY,
            scratch_shapes=[
                pltpu.VMEM((rows_all, C), BF16),
                pltpu.VMEM((2, rows_all, MB), BF16),
                pltpu.VMEM((2, MB, C), BF16),
                pltpu.VMEM((DONE * MB, C), BF16),
                pltpu.VMEM((MB, C), F32),
                DMA((4,)), DMA((2,)), DMA((2,)), DMA((2,)),
            ],
            compiler_params=params(),
            cost_estimate=pl.CostEstimate(flops=rows_all * D * C, bytes_accessed=80_000_000, transcendentals=0),
            name="matrix_gradient",
        )(g, xr, part)

        loss = jnp.concatenate([loss[j, :n] for j, n in enumerate(PS)])
        return loss, byx, by_w

    return jax.shard_map(
        step,
        mesh=mesh,
        in_specs=(P(("dp", "tp"), None), P(None, "tp"), P(("dp", "tp"))),
        out_specs=(P(("dp", "tp")), P(("dp", "tp"), None), P("dp", "tp")),
        check_vma=False,
    )
```

time: 589 us -> 359 us (0.61)
  Pallas kernels: 0 us -> 351 us
  matrix products: 244 us -> 0 us
  waiting for transfers between devices: 220 us -> 0 us
  other arithmetic: 56.6 us -> 0.67 us
  blocking collectives: 35.5 us -> 0 us
  between operations: 13.8 us -> 0.66 us
  local copies, waits for them, and re-layouts: 17.6 us -> 6.63 us
    pallas_call x0 -> x3, Pallas kernels: none -> 351 us  [the longest x1 164 us: step(): pl.pallas_call(second_kernel, out_shape=(S((R, D), BF16), S((rows_all, C)...]
    dot_general x3 -> x0, matrix products: 244 us -> none  [the longest x1 82.1 us: step(): logits = jnp.dot(rows, w, preferred_element_type=jnp.float32)]
    all_gather x2 -> x0, waiting for transfers between devices: 130 us -> none  [the longest x1 103 us: step(): rows = lax.all_gather(x, 'tp', axis=0, tiled=True)]
    reduce_scatter x1 -> x0, waiting for transfers between devices: 89.8 us -> none  [step(): by_x = lax.psum_scatter(term, 'tp', scatter_dimension=0, tiled=True)]
    unnamed x1 -> x0, blocking collectives: 35.5 us -> none
    convert_element_type x1 -> x0, other arithmetic: 29.1 us -> none  [step(): (e / total[:, None] - hit.astype(jnp.float32)).astype(jnp.bfloat16)]
    reduce_sum x2 -> x0, other arithmetic: 20.6 us -> none  [the longest x1 20.5 us: step(): jnp.sum(jnp.exp(logits - high[:, None]), -1)]
    unnamed x9 -> x1, local copies, waits for them, and re-layouts: 17.5 us -> 3.09 us
  transfers between devices with their start and end apart: 3 -> 0, of which waited for: 3 -> 0; matrix products, arithmetic and copies ran while one was open for 17% -> 0% of each run, Pallas kernels for 0% -> 0%
where the time goes in v1:
time: 359 us
  Pallas kernels  351 us (98%)
  local copies, waits for them, and re-layouts  6.63 us (2%)
    pallas_call x1, Pallas kernels, step(): pl.pallas_call(second_kernel, out_shape=(S((R, D), BF16), S((rows_all, C)...  164 us
    pallas_call x1, Pallas kernels, step(): pl.pallas_call(first_kernel, out_shape=(S((rows_all, C), F32), S((rows_al...  143 us
    pallas_call x1, Pallas kernels, step(): pl.pallas_call(third_kernel, out_shape=S((D, C), BF16), in_specs=[ANY, AN...  44.1 us

profile of v1, /device:TPU:0, one launch (start us, length us, event | category | flops | bytes accessed | tf_op | source)
XLA Modules:
  0.0 358.6 jit_solution(710903820573486891)
XLA Ops:
  0.6 0.7 slice_bitcast_fusion.3
  1.3 0.8 fusion
  2.2 0.6 pad.13.lab_ref
  2.8 142.5 %gather_logits.1 = (f32[5632,2048]{1,0:T(8,128)}, bf16[5632,3072]{1,0:T(8,128)(2,1)}, f32[8,128]{1,0:T(8,128)}, f32[16,8,128]{2,1,0:T(8,128)}, s32[16,8,128]{2,1,0:T(8,128)}) custom-call(bf16[352,3072]{1,0:T(8,128)(2,1)} %x_hbm.1, bf16[3072,2048]{1,0:T(8,128)(2,1)} %w_hbm.3, s32[8,128]{1,0:T(8,128)} %pad.13.lab_ref), custom_call_target="tpu_custom_call" | custom-call | flops 70866960384 | bytes 120000000 | tf_op jit(solution)/shard_map/gather_logits/pallas_call | solution.py:573
  145.3 0.7 slice_bitcast_fusion.2
  146.0 0.7 slice_bitcast_fusion.1
  146.7 0.7 pad_maximum_fusion
  147.4 164.0 %scatter_terms.1 = (bf16[352,3072]{1,0:T(8,128)(2,1)}, bf16[5632,2048]{1,0:T(8,128)(2,1)}, bf16[1536,2048]{1,0:T(8,128)(2,1)}, bf16[8,352,3072]{2,1,0:T(8,128)(2,1)}, bf16[8,352,3072]{2,1,0:T(8,128)(2,1)}) custom-call(f32[5632,2048]{1,0:T(8,128)} %get-tuple-element.12.z_hbm, bf16[5632,3072]{1,0:T(8,128)(2,1)} %get-tuple-element.13.xr_hbm, ...), custom_call_target="tpu_custom_call" | custom-call | flops 106300440576 | bytes 200000000 | tf_op jit(solution)/shard_map/scatter_terms/pallas_call | solution.py:604
  311.4 44.1 %matrix_gradient.1 = bf16[3072,2048]{1,0:T(8,128)(2,1)} custom-call(bf16[5632,2048]{1,0:T(8,128)(2,1)} %get-tuple-element.17.g_hbm, bf16[5632,3072]{1,0:T(8,128)(2,1)} %get-tuple-element.13.xr_hbm, bf16[1536,2048]{1,0:T(8,128)(2,1)} %get-tuple-element.18.part_hbm), custom_call_target="tpu_custom_call" | custom-call | flops 35433480192 | bytes 80000000 | tf_op jit(solution)/shard_map/matrix_gradient/pallas_call | solution.py:633
  355.5 3.1 copy.7
  (2 shorter events, 0.0 us)

commit v2 on v0

v2 whole, which is shorter than its diff:
```python
import jax
import jax.numpy as jnp
from jax import lax
from jax.experimental import pallas as pl
from jax.experimental.pallas import tpu as pltpu
from jax.sharding import PartitionSpec as P

F32, BF16, I32 = jnp.float32, jnp.bfloat16, jnp.int32
R, D, C = 352, 3072, 2048
H = R // 2
PO, PS = (0, 64, 128), (64, 64, 48)
AXES = (8, 4, 2)
NB = 16
MB = 256
DONE = 4
LAG = 10
VMEM_LIMIT = 67_000_000
THREE, TWO, PAIR = range(3), range(2), 2
LANES, Q = 128, 88
HALF_C, HALF_D = C // 2, D // 2


def flip(me, v):
    return v * (1 - 2 * ((me // v) % 2))


def place():
    me = lax.axis_index("tp")
    return me, me + flip(me, 1), [me + flip(me, v) for v in AXES]


def origin(me, s, k, j):
    q = me + k * flip(me, 1)
    for b in THREE:
        q = q + ((s // (1 << b)) % 2) * flip(me, AXES[(j + b) % 3])
    return q


def order(i):
    return jnp.where(i == 3, 4, jnp.where(i == 4, 3, i))


def rc(src, dst, ss, rs, dev):
    return pltpu.make_async_remote_copy(
        src_ref=src, dst_ref=dst, send_sem=ss, recv_sem=rs, device_id={"tp": dev}, device_id_type=pl.DeviceIdType.MESH
    )


def ds(start, size):
    return pl.ds(pl.multiple_of(start, 16), size)


def rows(j):
    return pl.ds(PO[j], PS[j])


def eye():
    return lax.broadcasted_iota(I32, (64, LANES), 0) == lax.broadcasted_iota(I32, (64, LANES), 1)


def to_column(row):
    return jnp.sum(jnp.where(eye(), row, 0.0), 1, keepdims=True)


def to_row(column, n):
    return jnp.sum(jnp.where(eye()[:n], column, 0.0), 0, keepdims=True)


def fill_columns(dst, k, tile, j, row, shift=0.0):
    put_column(dst, k, j, tile[pl.ds(row, 1), :].astype(F32) - shift)


def put_column(dst, k, j, row):
    col = to_column(row)
    dst[pl.ds(k * H + PO[j], PS[j]), :] = jnp.broadcast_to(col, (64, LANES))[: PS[j]]


def main_kernel(
    x_hbm, w_hbm, lab_ref,
    xr, z_hbm, loss_ref, g_hbm, bw, dbuf, ibuf, kept,
    w, g, acc, outd, outi, add, labc, c1, c2, c3, stile, strecv, st_all, lab_all,
    asend, arecv, adsend, adrecv, lsend, lrecv, ssend, srecv, tsend, trecv,
    dsend, drecv, isend, irecv, gsem, fsem, ksem, insem,
):
    me, partner, nbr = place()
    base = (me * C).astype(F32)
    barrier = pltpu.get_barrier_semaphore()

    def others(f):
        @pl.loop(1, NB)
        def _(t):
            f(t, (me + t) % NB)

    def own(h, b, j):
        n = h * 8 + (1 << b)
        return rc(
            x_hbm.at[ds(h * H + PO[j], PS[j])], xr.at[ds(n * R + PO[j], PS[j])],
            asend.at[n], arecv.at[n], nbr[(j + b) % 3],
        )

    def forward(h, s, b, j):
        n, t = h * 8 + s, h * 8 + s + (1 << b)
        return rc(
            xr.at[ds(n * R + PO[j], PS[j])], xr.at[ds(t * R + PO[j], PS[j])],
            asend.at[t], arecv.at[t], nbr[(j + b) % 3],
        )

    def pieces_of(n):
        return rc(xr.at[pl.ds(0, H)], xr.at[pl.ds(0, H)], asend.at[n], arecv.at[n], partner)

    def push(h, s):
        for b in (1, 2):

            @pl.when(s < (1 << b))
            def _():
                for j in THREE:
                    forward(h, s, b, j).start()

    def own_over(h):
        return rc(x_hbm.at[ds(h * H, H)], xr.at[ds(h * 8 * R + H, H)], adsend.at[h * 8], adrecv.at[h * 8], partner)

    def over(n):
        return rc(xr.at[ds(n * R, H)], xr.at[ds(n * R + H, H)], adsend.at[n], adrecv.at[n], partner)

    def label_copy(t, q):
        return rc(lab_ref, lab_all.at[me], lsend.at[0], lrecv.at[0], q)

    rest = pl.ds(0, NB - 1)

    def labels():
        return rc(lab_all.at[rest], lab_all.at[rest], lsend.at[0], lrecv.at[0], partner)

    def stat_copy(h, s, k, j):
        return rc(stile.at[h * 8 + s, k, j], strecv.at[h, me, j], ssend.at[h * 8 + s], srecv.at[h], origin(me, s, k, j))

    def top_copy(h, t, q):
        return rc(st_all.at[h, me], st_all.at[h, me], tsend.at[h], trecv.at[h], q)

    def tops(h):
        return rc(st_all.at[h, rest], st_all.at[h, rest], tsend.at[h], trecv.at[h], partner)

    def d2d(n, p):
        return rc(outd.at[p], dbuf.at[n], dsend.at[p], drecv.at[n], partner)

    def ici(n, b, p, j):
        return rc(outi.at[p, rows(j)], ibuf.at[n, rows(j)], isend.at[p], irecv.at[n], nbr[(j + b) % 3])

    def fetch(src, p):
        return pltpu.make_async_copy(src, add.at[p], fsem.at[p])

    def keep(h):
        return pltpu.make_async_copy(acc.at[1], kept.at[h], ksem.at[h])

    def g_out(n):
        return pltpu.make_async_copy(g.at[ds(n * R, R)], g_hbm.at[ds(n * R, R)], gsem.at[n])

    def wait_slot(n):
        rc(ibuf.at[n], ibuf.at[n], isend.at[0], irecv.at[n], partner).wait_recv()

    def wait_sent(p):
        rc(outi.at[p], ibuf.at[0], isend.at[p], irecv.at[0], partner).wait_send()

    def finish_start(v):
        s = 7 - order(v % 8)
        n = (v // 8) * 8 + s
        d2d(n, 0).wait_recv()
        fetch(dbuf.at[n], 0).start()

        @pl.when(s < 4)
        def _():
            wait_slot(n + 4)
            fetch(ibuf.at[n + 4], 1).start()

        @pl.when(s < 2)
        def _():
            wait_slot(n + 2)
            fetch(ibuf.at[n + 2], 2).start()

    def finish(v):
        s = 7 - order(v % 8)
        n = (v // 8) * 8 + s
        p = v % 3

        @pl.when(v > 2)
        def _():
            wait_sent(p)

        fetch(dbuf.at[n], 0).wait()

        def total(count):
            @pl.loop(0, H // 16)
            def _(i):
                r = pl.ds(pl.multiple_of(i * 16, 16), 16)
                out = acc[v % 2, r, :]
                for q in range(count):
                    out = out + add[q, r, :].astype(F32)
                outi[p, r, :] = out.astype(BF16)

        @pl.when(s >= 4)
        def _():
            total(1)
            for j in THREE:
                ici(n, 2, p, j).start()

        @pl.when(s < 4)
        def _():
            fetch(dbuf.at[n], 1).wait()

        @pl.when((s >= 2) & (s < 4))
        def _():
            total(2)
            for j in THREE:
                ici(n, 1, p, j).start()

        @pl.when(s == 1)
        def _():
            fetch(dbuf.at[n], 2).wait()
            total(3)
            for j in THREE:
                ici(n, 0, p, j).start()

    def combine(h):
        rc(strecv.at[h, rest], strecv.at[h, rest], ssend.at[0], srecv.at[h], partner).wait_recv()
        for j in THREE:
            tiles = [strecv[h, q, j] for q in range(NB)]
            top = tiles[0][0:1]
            for t in tiles[1:]:
                top = jnp.maximum(top, t[0:1])
            total = jnp.zeros((1, LANES), F32)
            right = jnp.zeros((1, LANES), F32)
            for t in tiles:
                total = total + t[1:2] * jnp.exp(t[0:1] - top)
                right = right + t[2:3]
            loss_ref[h, j : j + 1, :] = jnp.log(total) + top - right
            st_all[h, me, j : j + 1, :] = top
            st_all[h, me, j + 3 : j + 4, :] = 1.0 / total
        others(lambda t, q: top_copy(h, t, q).start())

    def passes(xbuf, zb, zin, xsem, zosem, zisem):
        def load_w(c):
            cols = pl.ds(pl.multiple_of(c * HALF_C, HALF_C), HALF_C)
            return pltpu.make_async_copy(w_hbm.at[:, cols], w.at[:, cols], insem.at[c])

        load_own = pltpu.make_async_copy(x_hbm, xbuf.at[1], insem.at[4])

        def put_own(h):
            return pltpu.make_async_copy(xbuf.at[1, pl.ds(h * H, H)], xr.at[ds(h * 8 * R, H)], insem.at[2 + h])

        def x_load(n, par):
            return pltpu.make_async_copy(xr.at[ds(n * R, R)], xbuf.at[par], xsem.at[par])

        def x_half(n, k, par):
            return pltpu.make_async_copy(xr.at[ds(n * R + k * H, H)], xbuf.at[par, pl.ds(k * H, H)], xsem.at[par])

        def z_out(n, par):
            return pltpu.make_async_copy(zb.at[par], z_hbm.at[ds(n * R, R)], zosem.at[par])

        def z_in(n, q):
            return pltpu.make_async_copy(z_hbm.at[pl.ds(pl.multiple_of(n * R + q * Q, 8), Q)], zin.at[q], zisem.at[q])

        load_own.start()
        first = pltpu.make_async_copy(x_hbm.at[pl.ds(0, H)], xbuf.at[0, pl.ds(0, H)], xsem.at[0])
        first.start()
        for c in TWO:
            load_w(c).start()
        others(lambda t, q: pl.semaphore_signal(barrier, inc=1, device_id={"tp": q}, device_id_type=pl.DeviceIdType.MESH))
        pl.semaphore_wait(barrier, NB - 1)
        own_over(0).start()
        others(lambda t, q: label_copy(t, q).start())
        for b in THREE:
            for j in THREE:
                own(0, b, j).start()
        lab_all[me] = lab_ref[...]
        load_own.wait()
        for h in TWO:
            put_own(h).start()
        own_over(0).wait_recv()
        pltpu.make_async_copy(xr.at[pl.ds(H, H)], xbuf.at[0, pl.ds(H, H)], xsem.at[0]).start()
        for h in TWO:
            put_own(h).wait()

        @pl.loop(0, 16 + LAG)
        def _(t):
            @pl.when(t < 16)
            def _():
                h = t // 8
                s = order(t % 8)
                n = h * 8 + s
                par = t % 2
                t1 = jnp.minimum(t + 1, 15)
                n1 = (t1 // 8) * 8 + order(t1 % 8)
                t2 = jnp.where(t < 7, t + 1, t + 2)
                h2 = jnp.minimum(t2 // 8, 1)
                s2 = order(t2 % 8)
                n2 = h2 * 8 + s2
                x_load(n, par).wait()

                @pl.when((t >= 7) & (t < 15))
                def _():
                    over(n1).wait_recv()
                    x_half(n1, 0, 1 - par).start()
                    x_half(n1, 1, 1 - par).start()

                @pl.when(t > 1)
                def _():
                    z_out(0, par).wait()

                @pl.when(t == 0)
                def _():
                    load_w(0).wait()
                    load_w(1).wait()

                @pl.loop(0, PAIR)
                def _(c):
                    cols = pl.ds(pl.multiple_of(c * HALF_C, HALF_C), HALF_C)
                    zb[par, :, cols] = jnp.dot(xbuf[par], w[:, cols], preferred_element_type=F32)

                @pl.when((t2 < 16) & (s2 > 0))
                def _():
                    pieces_of(n2).wait_recv()

                    @pl.when(t < 7)
                    def _():
                        push(h2, s2)
                        x_half(n1, 0, 1 - par).start()

                    over(n2).start()

                @pl.when(t == 5)
                def _():
                    own_over(1).start()
                    for j in THREE:
                        own(1, 0, j).start()

                @pl.when(t == 0)
                def _():
                    labels().wait_recv()

                for k in TWO:
                    for j in THREE:
                        fill_columns(labc, k, lab_all.at[origin(me, s, k, j)], j, h * 3 + j, base)

                @pl.loop(0, 4)
                def _(i):
                    r = pl.ds(pl.multiple_of(i * Q, 8), Q)
                    high = zb[par, r, 0:LANES]
                    for c in range(1, C // LANES):
                        high = jnp.maximum(high, zb[par, r, c * LANES : (c + 1) * LANES])
                    high = jnp.max(high, 1, keepdims=True)
                    lab = labc[r, :]
                    lane = lax.broadcasted_iota(I32, (1, LANES), 1).astype(F32)
                    sums = jnp.zeros((Q, LANES), F32)
                    right = jnp.zeros((Q, LANES), F32)
                    for c in range(C // LANES):
                        z = zb[par, r, c * LANES : (c + 1) * LANES]
                        e = jnp.exp(z - high)
                        hit = lane + float(c * LANES) == lab
                        sums = sums + e
                        right = right + jnp.where(hit, z, 0.0)
                        zb[par, r, c * LANES : (c + 1) * LANES] = jnp.where(hit, -1e-30 - e, e)
                    c1[r, :] = jnp.broadcast_to(high, (Q, LANES))
                    c2[r, :] = jnp.broadcast_to(jnp.sum(sums, 1, keepdims=True), (Q, LANES))
                    c3[r, :] = jnp.broadcast_to(jnp.sum(right, 1, keepdims=True), (Q, LANES))

                z_out(n, par).start()
                for k in TWO:
                    for j in THREE:
                        for i, ref in enumerate((c1, c2, c3)):
                            stile[n, k, j, i : i + 1, :] = to_row(ref[pl.ds(k * H + PO[j], PS[j]), :], PS[j])

                @pl.when(s == 0)
                def _():
                    for j in THREE:
                        strecv[h, me, j] = stile[n, 0, j]

                @pl.when(s > 0)
                def _():
                    for j in THREE:
                        stat_copy(h, s, 0, j).start()

                for j in THREE:
                    stat_copy(h, s, 1, j).start()

                @pl.when(t < 7)
                def _():
                    over(n1).wait_recv()
                    x_half(n1, 1, 1 - par).start()

            for b in (1, 2):

                @pl.when(t == 5 + b)
                def _():
                    for j in THREE:
                        own(1, b, j).start()

            @pl.when(t == 8)
            def _():
                combine(0)
                push(1, 1)

            @pl.when((t >= 8) & (t < 14))
            def _():
                push(1, order((t + 2) % 8))

            @pl.when(t == LAG - 1)
            def _():
                for i in range(4):
                    z_in(7, i).start()

            @pl.when(t == 16)
            def _():
                combine(1)
                z_out(0, 0).wait()
                z_out(0, 1).wait()

            @pl.when(t >= LAG)
            def _():
                u = t - LAG
                h = u // 8
                s = 7 - order(u % 8)
                n = h * 8 + s
                a = u % 2
                u2 = jnp.minimum(u + 1, 15)
                n2 = (u2 // 8) * 8 + 7 - order(u2 % 8)
                v = jnp.maximum(u - 1, 0)
                send_on = (u > 0) & (u != 8) & (u != 15)

                @pl.when(u % 8 == 0)
                def _():
                    tops(h).wait_recv()

                for k in TWO:
                    for j in THREE:
                        q = origin(me, s, k, j)
                        scale = jnp.exp(stile[n, k, j, 0:1, :] - st_all[h, q, j : j + 1, :]) * st_all[h, q, j + 3 : j + 4, :]
                        put_column(c1, k, j, scale)

                @pl.loop(0, 4)
                def _(i):
                    z_in(n, i).wait()
                    r = pl.ds(pl.multiple_of(i * Q, 8), Q)
                    to = pl.ds(pl.multiple_of(n * R + i * Q, 8), Q)
                    scale = c1[r, :]
                    for c in range(C // LANES):
                        e = zin[i, :, c * LANES : (c + 1) * LANES]
                        p = e * scale
                        g[to, c * LANES : (c + 1) * LANES] = jnp.where(e < 0.0, -1.0 - p, p).astype(BF16)

                    @pl.when(u < 15)
                    def _():
                        z_in(n2, i).start()

                g_out(n).start()

                @pl.when(u > 1)
                def _():
                    d2d(0, a).wait_send()

                @pl.when(u == 9)
                def _():
                    keep(0).wait()

                @pl.loop(0, PAIR)
                def _(c):
                    @pl.when((c == 1) & send_on)
                    def _():
                        finish_start(v)

                    cols = pl.ds(pl.multiple_of(c * HALF_D, HALF_D), HALF_D)
                    term = lax.dot_general(
                        g[ds(n * R, R), :], w[cols, :], (((1,), (1,)), ((), ())), preferred_element_type=F32
                    )
                    acc[a, :, cols] = term[:H]
                    outd[a, :, cols] = term[H:].astype(BF16)

                d2d(n, a).start()

                @pl.when(u % 8 == 7)
                def _():
                    keep(h).start()

                @pl.when(send_on)
                def _():
                    finish(v)

    def under(xb, ob, xsem, osem):
        def x_in(m):
            return pltpu.make_async_copy(xr.at[:, pl.ds(m * MB, MB)], xb.at[m % 2], xsem.at[m % 2])

        def bw_out(m):
            return pltpu.make_async_copy(ob.at[m % 2], bw.at[pl.ds(m * MB, MB)], osem.at[m % 2])

        x_in(0).start()
        x_in(1).start()

        finish_start(jnp.int32(14))

        @pl.loop(0, DONE)
        def _(m):
            x_in(m).wait()

            @pl.when(m > 1)
            def _():
                bw_out(m - 2).wait()

            by_w_block(xb.at[m % 2], g, ob.at[m % 2])
            bw_out(m).start()

            @pl.when(m + 2 < DONE)
            def _():
                x_in(m + 2).start()

            @pl.when(m == 0)
            def _():
                finish(jnp.int32(14))

        for m in (DONE - 2, DONE - 1):
            bw_out(m).wait()

    sem = pltpu.SemaphoreType.DMA
    pl.run_scoped(passes, pltpu.VMEM((2, R, D), BF16), pltpu.VMEM((2, R, C), F32), pltpu.VMEM((4, Q, C), F32), sem((2,)), sem((2,)), sem((4,)))
    pl.run_scoped(under, pltpu.VMEM((2, NB * R, MB), BF16), pltpu.VMEM((2, MB, C), BF16), sem((2,)), sem((2,)))

    for a in TWO:
        d2d(0, a).wait_send()
    keep(1).wait()
    for h in TWO:
        d2d(h * 8, 0).wait_recv()
        for s in (1, 2, 4):
            wait_slot(h * 8 + s)

    for p in THREE:
        wait_sent(p)

    @pl.loop(0, 16)
    def _(n):
        g_out(n).wait()
        over(n).wait_send()

        @pl.when(n % 8 > 0)
        def _():
            pieces_of(n).wait_send()
            rc(stile.at[n], stile.at[n], ssend.at[n], srecv.at[0], partner).wait_send()

        @pl.when(n % 8 == 0)
        def _():
            rc(stile.at[n, 1], stile.at[n, 1], ssend.at[n], srecv.at[0], partner).wait_send()

    labels().wait_send()
    for h in TWO:
        tops(h).wait_send()


def by_w_block(xb, g, ob):
    for c in range(4):
        ob[:, c * 512 : (c + 1) * 512] = lax.dot_general(
            xb[...], g[:, c * 512 : (c + 1) * 512], (((0,), (0,)), ((), ())), preferred_element_type=F32
        ).astype(BF16)


def third_kernel(
    g_hbm, xr_hbm, part_hbm, kept, dbuf, ibuf,
    bw, byx,
    g, xb, ob, part, acc, sums, add, gsem, x0sem, xsem, osem, psem, fsem, ysem,
):
    blocks = D // MB
    cuts = ((0, 512), (512, 1024), (1536, 2048), (3584, 2048))

    def g_in(n):
        r = pl.ds(*cuts[n])
        return pltpu.make_async_copy(g_hbm.at[r], g.at[r], gsem.at[n])

    def x_cut(i, n):
        r = pl.ds(*cuts[n])
        return pltpu.make_async_copy(xr_hbm.at[r, pl.ds((DONE + i) * MB, MB)], xb.at[i, r], x0sem.at[i, n])

    def x_in(m):
        return pltpu.make_async_copy(xr_hbm.at[:, pl.ds(m * MB, MB)], xb.at[m % 2], xsem.at[m % 2])

    def bw_out(m):
        return pltpu.make_async_copy(ob.at[m % 2], bw.at[pl.ds(m * MB, MB)], osem.at[m % 2])

    p_in = pltpu.make_async_copy(part_hbm, part, psem.at[0])
    p_out = pltpu.make_async_copy(part, bw.at[pl.ds(0, DONE * MB)], psem.at[1])
    came = [pltpu.make_async_copy(kept, sums, fsem.at[8])]
    for h in TWO:
        came.append(pltpu.make_async_copy(dbuf.at[h * 8], add.at[h, 0], fsem.at[h * 4]))
        for p, n in enumerate((1, 2, 4)):
            came.append(pltpu.make_async_copy(ibuf.at[h * 8 + n], add.at[h, p + 1], fsem.at[h * 4 + p + 1]))
    y_out = [pltpu.make_async_copy(add.at[h, 0], byx.at[pl.ds(h * H, H)], ysem.at[h]) for h in TWO]

    def begin(n):
        for i in TWO:
            x_cut(i, n).start()
        g_in(n).start()

    begin(0)
    begin(1)
    for n in range(4):
        r = pl.ds(*cuts[n])
        for i in TWO:
            x_cut(i, n).wait()
        g_in(n).wait()
        if n < 2:
            begin(n + 2)
        for i in TWO:

            @pl.loop(0, PAIR)
            def _(c):
                cols = pl.ds(pl.multiple_of(c * HALF_C, HALF_C), HALF_C)
                t = lax.dot_general(xb[i, r, :], g[r, cols], (((0,), (0,)), ((), ())), preferred_element_type=F32)
                if n == 0:
                    acc[i, :, cols] = t
                elif n < 3:
                    acc[i, :, cols] += t
                else:
                    ob[i, :, cols] = (acc[i, :, cols] + t).astype(BF16)

            if n == 3:
                bw_out(DONE + i).start()
                x_in(DONE + 2 + i).start()
    p_in.start()
    for copy in came:
        copy.start()

    @pl.loop(DONE + 2, blocks)
    def _(m):
        x_in(m).wait()
        bw_out(m - 2).wait()
        by_w_block(xb.at[m % 2], g, ob.at[m % 2])
        bw_out(m).start()

        @pl.when(m + 2 < blocks)
        def _():
            x_in(m + 2).start()

        @pl.when(m == DONE + 4)
        def _():
            p_in.wait()
            p_out.start()
            for copy in came:
                copy.wait()
            for h in TWO:

                @pl.loop(0, H // 16)
                def _(i):
                    r = pl.ds(pl.multiple_of(i * 16, 16), 16)
                    out = sums[h, r, :]
                    for p in range(4):
                        out = out + add[h, p, r, :].astype(F32)
                    add[h, 0, r, :] = out.astype(BF16)

                y_out[h].start()

    for m in (blocks - 2, blocks - 1):
        bw_out(m).wait()
    p_out.wait()
    for copy in y_out:
        copy.wait()


ANY = pl.BlockSpec(memory_space=pl.ANY)
VM = pl.BlockSpec(memory_space=pltpu.VMEM)


def params(n=None):
    if n is None:
        return pltpu.CompilerParams(vmem_limit_bytes=VMEM_LIMIT)
    return pltpu.CompilerParams(vmem_limit_bytes=VMEM_LIMIT, collective_id=n, has_side_effects=True)


def S(shape, dtype):
    return jax.ShapeDtypeStruct(shape, dtype)


def pieces(v):
    v = jnp.pad(v.reshape(2, H), ((0, 0), (0, 16))).reshape(6, 64)
    return jnp.pad(v, ((0, 2), (0, 64)))


def solution(mesh):
    DMA = pltpu.SemaphoreType.DMA
    rows_all = NB * R

    def step(x, w, label):
        xr, _, loss, g, part, dbuf, ibuf, kept = pl.pallas_call(
            main_kernel,
            out_shape=(
                S((rows_all, D), BF16),
                S((rows_all, C), F32),
                S((2, 8, LANES), F32),
                S((rows_all, C), BF16),
                S((DONE * MB, C), BF16),
                S((16, H, D), BF16),
                S((16, H, D), BF16),
                S((2, H, D), F32),
            ),
            in_specs=[ANY, ANY, VM],
            out_specs=(ANY, ANY, VM, ANY, ANY, ANY, ANY, ANY),
            scratch_shapes=[
                pltpu.VMEM((D, C), BF16),
                pltpu.VMEM((rows_all, C), BF16),
                pltpu.VMEM((2, H, D), F32),
                pltpu.VMEM((2, H, D), BF16),
                pltpu.VMEM((3, H, D), BF16),
                pltpu.VMEM((3, H, D), BF16),
                pltpu.VMEM((R, LANES), F32),
                pltpu.VMEM((R, LANES), F32),
                pltpu.VMEM((R, LANES), F32),
                pltpu.VMEM((R, LANES), F32),
                pltpu.VMEM((16, 2, 3, 8, LANES), F32),
                pltpu.VMEM((2, NB, 3, 8, LANES), F32),
                pltpu.VMEM((2, NB, 8, LANES), F32),
                pltpu.VMEM((NB, 8, LANES), I32),
                *[DMA((n,)) for n in (16, 16, 16, 16, 1, 1, 16, 2, 2, 2, 2, 16, 3, 16)], DMA((16,)), DMA((3,)), DMA((2,)), DMA((5,)),
            ],
            compiler_params=params(0),
            cost_estimate=pl.CostEstimate(flops=5 * rows_all * D * C, bytes_accessed=300_000_000, transcendentals=2 * rows_all * C),
            name="gather_logits_terms",
        )(x, w, pieces(label))

        by_w, byx = pl.pallas_call(
            third_kernel,
            out_shape=(S((D, C), BF16), S((R, D), BF16)),
            in_specs=[ANY] * 6,
            out_specs=(ANY, ANY),
            scratch_shapes=[
                pltpu.VMEM((rows_all, C), BF16),
                pltpu.VMEM((2, rows_all, MB), BF16),
                pltpu.VMEM((2, MB, C), BF16),
                pltpu.VMEM((DONE * MB, C), BF16),
                pltpu.VMEM((2, MB, C), F32),
                pltpu.VMEM((2, H, D), F32),
                pltpu.VMEM((2, 4, H, D), BF16),
                DMA((4,)), DMA((2, 4)), DMA((2,)), DMA((2,)), DMA((2,)), DMA((9,)), DMA((2,)),
            ],
            compiler_params=params(),
            cost_estimate=pl.CostEstimate(flops=rows_all * D * C, bytes_accessed=80_000_000, transcendentals=0),
            name="matrix_gradient",
        )(g, xr, part, kept, dbuf, ibuf)

        loss = loss[:, :3, :64].reshape(2, 192)[:, :H].reshape(R)
        return loss, byx, by_w

    return jax.shard_map(
        step,
        mesh=mesh,
        in_specs=(P(("dp", "tp"), None), P(None, "tp"), P(("dp", "tp"))),
        out_specs=(P(("dp", "tp")), P(("dp", "tp"), None), P("dp", "tp")),
        check_vma=False,
    )
```

time: 589 us -> 324 us (0.55)
  Pallas kernels: 0 us -> 320 us
  matrix products: 244 us -> 0 us
  waiting for transfers between devices: 220 us -> 0 us
  other arithmetic: 56.6 us -> 0 us
  blocking collectives: 35.5 us -> 0 us
  local copies, waits for them, and re-layouts: 17.6 us -> 2.9 us
  between operations: 13.8 us -> 0.8 us
    pallas_call x0 -> x2, Pallas kernels: none -> 320 us  [the longest x1 264 us: step(): pl.pallas_call(main_kernel, out_shape=(S((rows_all, D), BF16), S((rows_al...]
    dot_general x3 -> x0, matrix products: 244 us -> none  [the longest x1 82.1 us: step(): logits = jnp.dot(rows, w, preferred_element_type=jnp.float32)]
    all_gather x2 -> x0, waiting for transfers between devices: 130 us -> none  [the longest x1 103 us: step(): rows = lax.all_gather(x, 'tp', axis=0, tiled=True)]
    reduce_scatter x1 -> x0, waiting for transfers between devices: 89.8 us -> none  [step(): by_x = lax.psum_scatter(term, 'tp', scatter_dimension=0, tiled=True)]
    unnamed x1 -> x0, blocking collectives: 35.5 us -> none
    convert_element_type x1 -> x0, other arithmetic: 29.1 us -> none  [step(): (e / total[:, None] - hit.astype(jnp.float32)).astype(jnp.bfloat16)]
    reduce_sum x2 -> x0, other arithmetic: 20.6 us -> none  [the longest x1 20.5 us: step(): jnp.sum(jnp.exp(logits - high[:, None]), -1)]
    unnamed x9 -> x0, local copies, waits for them, and re-layouts: 17.5 us -> none
  transfers between devices with their start and end apart: 3 -> 0, of which waited for: 3 -> 0; matrix products, arithmetic and copies ran while one was open for 17% -> 0% of each run, Pallas kernels for 0% -> 0%
where the time goes in v2:
time: 324 us
  Pallas kernels  320 us (99%)
    pallas_call x1, Pallas kernels, step(): pl.pallas_call(main_kernel, out_shape=(S((rows_all, D), BF16), S((rows_al...  264 us
    pallas_call x1, Pallas kernels, step(): pl.pallas_call(third_kernel, out_shape=(S((D, C), BF16), S((R, D), BF16))...  56.4 us

profile of v2, /device:TPU:0, one launch (start us, length us, event | category | flops | bytes accessed | tf_op | source)
XLA Modules:
  0.0 323.7 jit_solution(15872507356112799274)
XLA Ops:
  0.6 0.8 reshape.18
  1.4 0.1 reshape.19
  1.5 0.6 pad.9.lab_ref
  2.1 263.6 %gather_logits_terms.1 = (bf16[5632,3072]{1,0:T(8,128)(2,1)}, f32[5632,2048]{1,0:T(8,128)}, f32[2,8,128]{2,1,0:T(8,128)}, bf16[5632,2048]{1,0:T(8,128)(2,1)}, bf...) custom-call(bf16[352,3072]{1,0:T(8,128)(2,1)} %x_hbm.1, ...), custom_call_target="tpu_custom_call" | custom-call | flops 177167400960 | bytes 300000000 | tf_op jit(solution)/shard_map/gather_logits_terms/pallas_call | solution.py:686
  265.7 0.7 slice.6
  266.4 0.1 reshape.20
  266.4 0.7 reshape.21
  267.1 56.4 %matrix_gradient.1 = (bf16[3072,2048]{1,0:T(8,128)(2,1)}, bf16[352,3072]{1,0:T(8,128)(2,1)}) custom-call(bf16[5632,2048]{1,0:T(8,128)(2,1)} %get-tuple-element.13.g_hbm, bf16[5632,3072]{1,0:T(8,128)(2,1)} %get-tuple-element.14.xr_hbm, bf16[1024,2048]{1,0:T(8,128)(2,1)} %get-tuple-element.15.part_hbm, f32[2,176,3072]{2,1,0:T(8,128)} %get-tuple-element.16.kept, ...), custom_call_target="tpu_custom_call" | custom-call | flops 35433480192 | bytes 80000000 | tf_op jit(solution)/shard_map/matrix_gradient/pallas_call | solution.py:722
  (1 shorter events, 0.0 us)
